TPU v7x, 32 devices: a whole 2x2x4 slice. The times are simulated.
32 devices in a mesh: dp: 4 (over x, core), pipe: 2 (over y), tensor: 4 (over z).
Axes of the slice: x: 2, y: 2, z: 4, core: 2. Of those that a mesh axis runs over, the one named last changes fastest.
Arguments:
- weights: bfloat16 [2816, 1408], P(('dp', 'pipe', 'tensor')), may hold values from -6 to 6
- first_moment: bfloat16 [2816, 1408], P(('dp', 'pipe', 'tensor')), may hold values from -6 to 6
- second_moment: bfloat16 [2816, 1408], P(('dp', 'pipe', 'tensor')), may hold values from 0.049804688 to 5
- row_weight: float32 [1408], replicated, may hold values from -1 to 1
- col_weight: float32 [1408], replicated, may hold values from 1 to 4
Outputs:
- weight_tiles: bfloat16 [2816, 1408], P(('pipe', 'tensor'))
- first_tiles: bfloat16 [2816, 1408], P(('pipe', 'tensor'))
- second_tiles: bfloat16 [2816, 1408], P(('pipe', 'tensor'))
- checksums: float32 [3, 2, 4, 11], P(None, 'pipe', 'tensor')
All inputs are finite; a program needn't handle non-finite values.
Results may differ from a plain program's by a relative error of at most 0.001.
Values may be sent and summed in bfloat16 or wider, within the bound.
A program may use at most 64 MiB of HBM per device.

v0:
```python
import jax
import jax.numpy as jnp
from jax import lax
from jax.sharding import PartitionSpec as P

CHECK_COLS = 128


def for_sending(array):
    return jax.tree.map(lambda a: a.astype(jnp.bfloat16) if a.dtype == jnp.float32 else a, array)


def column_sums(data, row_part, col_weight, col_blocks):
    row_mixed = jnp.dot(
        row_part[None, :], data.astype(jnp.float32), precision=lax.Precision.HIGHEST
    )[0]
    return jnp.sum((row_mixed * col_weight).reshape(col_blocks, -1), axis=1)


def shards(weights, first_moment, second_moment, row_weight, col_weight):
    dp_count = lax.axis_size("dp")
    pipe_count = lax.axis_size("pipe")
    tensor_count = lax.axis_size("tensor")
    shard_rows, width = weights.shape
    dp_section = dp_count // pipe_count
    tile_shards = dp_count // tensor_count
    piece_cols = width // dp_count
    tile_rows = shard_rows * dp_count
    col_blocks = width // CHECK_COLS
    factor = float(tile_rows * CHECK_COLS) ** (-0.5)
    sources = (weights, first_moment, second_moment)
    exchanged = (
        lax.all_to_all(sources[0], "dp", split_axis=1, concat_axis=0, tiled=True),
        lax.all_to_all(sources[1], "dp", split_axis=1, concat_axis=0, tiled=True),
        lax.all_to_all(sources[2], "dp", split_axis=1, concat_axis=0, tiled=True),
    )
    grouped = tuple(
        (item.reshape(pipe_count, dp_section, shard_rows, piece_cols) for item in exchanged)
    )
    sectioned = jax.tree.map(
        lambda part, own: part.astype(own.dtype),
        lax.all_to_all(for_sending(grouped), "pipe", split_axis=0, concat_axis=2, tiled=True),
        grouped,
    )
    routed = tuple(
        (item.reshape(tensor_count, tile_shards, 1, shard_rows, piece_cols) for item in sectioned)
    )
    arrived = jax.tree.map(
        lambda part, own: part.astype(own.dtype),
        lax.all_to_all(for_sending(routed), "tensor", split_axis=0, concat_axis=2, tiled=True),
        routed,
    )
    flat_pieces = tuple((item.reshape(tile_rows, piece_cols) for item in arrived))
    tiles = jax.tree.map(
        lambda part, own: part.astype(own.dtype),
        lax.all_gather(for_sending(flat_pieces), "dp", axis=1, tiled=True),
        flat_pieces,
    )
    tensor_pos = lax.axis_index("tensor")
    flat_index = (
        lax.axis_index("dp") * pipe_count + lax.axis_index("pipe")
    ) * tensor_count + tensor_pos
    in_section = flat_index % (dp_count * tensor_count)
    section_of = flat_index // (dp_count * tensor_count)
    tile_of = in_section // dp_count
    row_part = lax.dynamic_slice_in_dim(row_weight, in_section * shard_rows, shard_rows)
    partial_value = jnp.stack(
        [column_sums(item, row_part, col_weight, col_blocks) for item in sources]
    )
    section_hit = (jnp.arange(pipe_count) == section_of).astype(jnp.float32)
    tile_hit = (jnp.arange(tensor_count) == tile_of).astype(jnp.float32)
    spread = (
        partial_value[:, None, None, :]
        * section_hit[None, :, None, None]
        * tile_hit[None, None, :, None]
    )
    summed = lax.psum(spread, ("dp", "pipe", "tensor"))
    checks = (
        lax.dynamic_slice(summed, (0, lax.axis_index("pipe"), tensor_pos, 0), (3, 1, 1, col_blocks))
        * factor
    )
    return (tiles[0], tiles[1], tiles[2], checks)


def solution(mesh):
    return jax.shard_map(
        shards,
        mesh=mesh,
        in_specs=(
            P(("dp", "pipe", "tensor"), None),
            P(("dp", "pipe", "tensor"), None),
            P(("dp", "pipe", "tensor"), None),
            P(),
            P(),
        ),
        out_specs=(
            P(("pipe", "tensor"), None),
            P(("pipe", "tensor"), None),
            P(("pipe", "tensor"), None),
            P(None, "pipe", "tensor", None),
        ),
        check_vma=False,
    )
```

profile of v0, /device:TPU:0, one launch (start us, length us, event | category | flops | bytes accessed | tf_op | source)
XLA Modules:
  0.0 154.1 jit_solution(8427268718347811385)
XLA Ops:
  0.6 0.0 copy-start
  0.6 0.0 copy-start.3
  0.7 1.3 all_to_all.90
  1.9 0.7 copy.33
  2.7 4.4 %all-to-all-start = ((bf16[88,4,352]{2,0,1:T(8,128)(2,1)}), bf16[88,4,352]{2,0,1:T(8,128)(2,1)}, u32[]{:S(2)}, u32[]{:S(2)}) async-start(bf16[88,4,352]{2,0,1:T(8,128)(2,1)} %copy.33), calls=%async_computation | async-start | bytes 540672 | tf_op jit(solution)/shard_map/all_to_all | solution.py:33
  7.0 0.0 copy-done.3
  7.0 0.3 all_to_all.97
  7.3 0.7 copy.37
  8.1 5.6 %all-to-all-done = bf16[88,4,352]{2,0,1:T(8,128)(2,1)} async-done(((bf16[88,4,352]{2,0,1:T(8,128)(2,1)}), bf16[88,4,352]{2,0,1:T(8,128)(2,1)}, u32[]{:S(2)}, u32[]{:S(2)}) %all-to-all-start) | async-done | bytes 247840 | tf_op jit(solution)/shard_map/all_to_all | solution.py:33
  13.7 4.1 %all-to-all-start.3 = ((bf16[88,4,352]{2,0,1:T(8,128)(2,1)}), bf16[88,4,352]{2,0,1:T(8,128)(2,1)}, u32[]{:S(2)}, u32[]{:S(2)}) async-start(bf16[88,4,352]{2,0,1:T(8,128)(2,1)} %copy.37), calls=%async_computation.3 | async-start | bytes 540672 | tf_op jit(solution)/shard_map/all_to_all | solution.py:34
  17.8 0.3 all_to_all.104
  18.1 0.0 copy-start.4
  18.1 0.7 copy.41
  18.9 5.1 %all-to-all-done.3 = bf16[88,4,352]{2,0,1:T(8,128)(2,1)} async-done(((bf16[88,4,352]{2,0,1:T(8,128)(2,1)}), bf16[88,4,352]{2,0,1:T(8,128)(2,1)}, u32[]{:S(2)}, u32[]{:S(2)}) %all-to-all-start.3) | async-done | bytes 247840 | tf_op jit(solution)/shard_map/all_to_all | solution.py:34
  24.0 4.1 %all-to-all-start.6 = ((bf16[88,4,352]{2,0,1:T(8,128)(2,1)}), bf16[88,4,352]{2,0,1:T(8,128)(2,1)}, u32[]{:S(2)}, u32[]{:S(2)}) async-start(bf16[88,4,352]{2,0,1:T(8,128)(2,1)} %copy.41), calls=%async_computation.6 | async-start | bytes 540672 | tf_op jit(solution)/shard_map/all_to_all | solution.py:35
  28.1 0.3 convolution_reduce_fusion.2
  28.4 0.3 convolution_reduce_fusion
  28.7 5.5 %all-to-all-done.6 = bf16[88,4,352]{2,0,1:T(8,128)(2,1)} async-done(((bf16[88,4,352]{2,0,1:T(8,128)(2,1)}), bf16[88,4,352]{2,0,1:T(8,128)(2,1)}, u32[]{:S(2)}, u32[]{:S(2)}) %all-to-all-start.6) | async-done | bytes 247840 | tf_op jit(solution)/shard_map/all_to_all | solution.py:35
  34.2 3.6 %all-to-all-start.1 = ((bf16[2,2,88,352]{3,2,1,0:T(8,128)(2,1)}), bf16[2,2,88,352]{3,2,1,0:T(8,128)(2,1)S(1)}, u32[]{:S(2)}, u32[]{:S(2)}) async-start(bf16[2,2,88,352]{3,2,1,0:T(8,128)(2,1)} %bitcast.1), calls=%async_computation.1 | async-start | bytes 540672 | tf_op jit(solution)/shard_map/all_to_all | solution.py:42
  37.8 0.3 convolution_reduce_fusion.1
  38.1 0.1 bitcast_reduce_fusion.2
  38.3 5.2 %all-to-all-done.1 = bf16[2,2,88,352]{3,2,1,0:T(8,128)(2,1)S(1)} async-done(((bf16[2,2,88,352]{3,2,1,0:T(8,128)(2,1)}), bf16[2,2,88,352]{3,2,1,0:T(8,128)(2,1)S(1)}, u32[]{:S(2)}, u32[]{:S(2)}) %all-to-all-start.1) | async-done | bytes 247840 | tf_op jit(solution)/shard_map/all_to_all | solution.py:42
  43.5 3.4 %all-to-all-start.4 = ((bf16[2,2,88,352]{3,2,1,0:T(8,128)(2,1)}), bf16[2,2,88,352]{3,2,1,0:T(8,128)(2,1)S(1)}, u32[]{:S(2)}, u32[]{:S(2)}) async-start(bf16[2,2,88,352]{3,2,1,0:T(8,128)(2,1)} %bitcast.8), calls=%async_computation.4 | async-start | bytes 540672 | tf_op jit(solution)/shard_map/all_to_all | solution.py:42
  47.0 5.2 %all-to-all-done.4 = bf16[2,2,88,352]{3,2,1,0:T(8,128)(2,1)S(1)} async-done(((bf16[2,2,88,352]{3,2,1,0:T(8,128)(2,1)}), bf16[2,2,88,352]{3,2,1,0:T(8,128)(2,1)S(1)}, u32[]{:S(2)}, u32[]{:S(2)}) %all-to-all-start.4) | async-done | bytes 247840 | tf_op jit(solution)/shard_map/all_to_all | solution.py:42
  52.1 3.4 %all-to-all-start.7 = ((bf16[2,2,88,352]{3,2,1,0:T(8,128)(2,1)}), bf16[2,2,88,352]{3,2,1,0:T(8,128)(2,1)S(1)}, u32[]{:S(2)}, u32[]{:S(2)}) async-start(bf16[2,2,88,352]{3,2,1,0:T(8,128)(2,1)} %bitcast.15), calls=%async_computation.7 | async-start | bytes 540672 | tf_op jit(solution)/shard_map/all_to_all | solution.py:42
  55.6 0.1 broadcast_multiply_fusion.1
  55.6 0.7 copy.34
  56.4 4.4 %all-to-all-done.7 = bf16[2,2,88,352]{3,2,1,0:T(8,128)(2,1)S(1)} async-done(((bf16[2,2,88,352]{3,2,1,0:T(8,128)(2,1)}), bf16[2,2,88,352]{3,2,1,0:T(8,128)(2,1)S(1)}, u32[]{:S(2)}, u32[]{:S(2)}) %all-to-all-start.7) | async-done | bytes 247840 | tf_op jit(solution)/shard_map/all_to_all | solution.py:42
  60.8 5.1 %all-to-all-start.2 = ((bf16[4,1,1,88,352]{4,3,2,1,0:T(8,128)(2,1)}), bf16[4,1,1,88,352]{4,3,2,1,0:T(8,128)(2,1)S(1)}, u32[]{:S(2)}, u32[]{:S(2)}) async-start(bf16[4,1,1,88,352]{4,3,2,1,0:T(8,128)(2,1)} %bitcast.5), calls=%async_computation.2 | async-start | bytes 540672 | tf_op jit(solution)/shard_map/all_to_all | solution.py:50
  65.9 0.1 broadcast_multiply_fusion
  65.9 39.9 %psum.7 = f32[3,2,4,11]{3,2,1,0:T(4,128)S(1)} all-reduce(f32[3,2,4,11]{3,2,1,0:T(4,128)S(1)} %broadcast_multiply_fusion), channel_id=1, replica_groups=mesh['dp'=4,'pipe'=2,'tensor'=4] {'dp','pipe','tensor'}, use_global_device_ids=true, to_apply=%region_3.4 | all-reduce | flops 264 | bytes 2112 | tf_op jit(solution)/shard_map/psum | solution.py:77
  105.8 0.6 dynamic-slice_multiply_fusion
  106.4 0.7 copy.38
  107.1 0.7 copy.42
  107.9 0.0 all-to-all-done.2
  107.9 3.6 %all-to-all-start.5 = ((bf16[4,1,1,88,352]{4,3,2,1,0:T(8,128)(2,1)}), bf16[4,1,1,88,352]{4,3,2,1,0:T(8,128)(2,1)S(1)}, u32[]{:S(2)}, u32[]{:S(2)}) async-start(bf16[4,1,1,88,352]{4,3,2,1,0:T(8,128)(2,1)} %bitcast.12), calls=%async_computation.5 | async-start | bytes 540672 | tf_op jit(solution)/shard_map/all_to_all | solution.py:50
  111.4 0.2 copy.36
  111.6 11.0 %all_gather.9 = bf16[352,1408]{0,1:T(8,128)(2,1)S(1)} all-gather(bf16[352,352]{0,1:T(8,128)(2,1)S(1)} %copy.36), channel_id=1, replica_groups=mesh['dp'=4,'pipe'=2,'tensor'=4] {'dp'}, dimensions={1}, use_global_device_ids=true | all-gather | bytes 1239040 | tf_op jit(solution)/shard_map/all_gather | solution.py:56
  122.6 1.9 %copy.45 = bf16[352,1408]{1,0:T(8,128)(2,1)} copy(bf16[352,1408]{0,1:T(8,128)(2,1)S(1)} %all_gather.9) | data formatting | bytes 1982464
  124.5 0.0 all-to-all-done.5
  124.5 5.1 %all-to-all-start.8 = ((bf16[4,1,1,88,352]{4,3,2,1,0:T(8,128)(2,1)}), bf16[4,1,1,88,352]{4,3,2,1,0:T(8,128)(2,1)S(1)}, u32[]{:S(2)}, u32[]{:S(2)}) async-start(bf16[4,1,1,88,352]{4,3,2,1,0:T(8,128)(2,1)} %bitcast.19), calls=%async_computation.8 | async-start | bytes 540672 | tf_op jit(solution)/shard_map/all_to_all | solution.py:50
  129.6 0.2 copy.40
  129.8 10.0 %all_gather.10 = bf16[352,1408]{0,1:T(8,128)(2,1)S(1)} all-gather(bf16[352,352]{0,1:T(8,128)(2,1)S(1)} %copy.40), channel_id=1, replica_groups=mesh['dp'=4,'pipe'=2,'tensor'=4] {'dp'}, dimensions={1}, use_global_device_ids=true | all-gather | bytes 1239040 | tf_op jit(solution)/shard_map/all_gather | solution.py:56
  139.8 1.9 %copy.46 = bf16[352,1408]{1,0:T(8,128)(2,1)} copy(bf16[352,1408]{0,1:T(8,128)(2,1)S(1)} %all_gather.10) | data formatting | bytes 1982464
  141.7 0.0 all-to-all-done.8
  141.7 0.2 copy.44
  141.9 10.3 %all_gather.11 = bf16[352,1408]{0,1:T(8,128)(2,1)S(1)} all-gather(bf16[352,352]{0,1:T(8,128)(2,1)S(1)} %copy.44), channel_id=1, replica_groups=mesh['dp'=4,'pipe'=2,'tensor'=4] {'dp'}, dimensions={1}, use_global_device_ids=true | all-gather | bytes 1239040 | tf_op jit(solution)/shard_map/all_gather | solution.py:56
  152.2 1.9 %copy.47 = bf16[352,1408]{1,0:T(8,128)(2,1)} copy(bf16[352,1408]{0,1:T(8,128)(2,1)S(1)} %all_gather.11) | data formatting | bytes 1982464
  (9 shorter events, 0.0 us)
Async XLA Ops:
  0.6 27.4 %copy-start = (f32[1408]{0:T(1024)S(1)}, f32[1408]{0:T(1024)}, u32[]{:S(2)}) copy-start(f32[1408]{0:T(1024)} %param.8) | copy-start | bytes 16900
  0.6 6.4 %copy-start.3 = (bf16[88,1408]{1,0:T(8,128)(2,1)S(1)}, bf16[88,1408]{1,0:T(8,128)(2,1)}, u32[]{:S(2)}) copy-start(bf16[88,1408]{1,0:T(8,128)(2,1)} %param.6) | copy-start | bytes 743428
  2.7 15.2 %copy-start.2 = (bf16[88,1408]{1,0:T(8,128)(2,1)S(1)}, bf16[88,1408]{1,0:T(8,128)(2,1)}, u32[]{:S(2)}) copy-start(bf16[88,1408]{1,0:T(8,128)(2,1)} %param.7) | copy-start | bytes 743428
  2.7 11.0 %all-to-all-start = ((bf16[88,4,352]{2,0,1:T(8,128)(2,1)}), bf16[88,4,352]{2,0,1:T(8,128)(2,1)}, u32[]{:S(2)}, u32[]{:S(2)}) async-start(bf16[88,4,352]{2,0,1:T(8,128)(2,1)} %copy.33), calls=%async_computation | async-start | bytes 540672 | tf_op jit(solution)/shard_map/all_to_all | solution.py:33
  8.1 20.0 %copy-start.1 = (bf16[88,1408]{1,0:T(8,128)(2,1)S(1)}, bf16[88,1408]{1,0:T(8,128)(2,1)}, u32[]{:S(2)}) copy-start(bf16[88,1408]{1,0:T(8,128)(2,1)} %param.5) | copy-start | bytes 743428
  13.7 10.2 %all-to-all-start.3 = ((bf16[88,4,352]{2,0,1:T(8,128)(2,1)}), bf16[88,4,352]{2,0,1:T(8,128)(2,1)}, u32[]{:S(2)}, u32[]{:S(2)}) async-start(bf16[88,4,352]{2,0,1:T(8,128)(2,1)} %copy.37), calls=%async_computation.3 | async-start | bytes 540672 | tf_op jit(solution)/shard_map/all_to_all | solution.py:34
  18.1 20.0 %copy-start.4 = (f32[1408]{0:T(1024)S(1)}, f32[1408]{0:T(1024)}, u32[]{:S(2)}) copy-start(f32[1408]{0:T(1024)} %param.9) | copy-start | bytes 16900
  24.0 10.2 %all-to-all-start.6 = ((bf16[88,4,352]{2,0,1:T(8,128)(2,1)}), bf16[88,4,352]{2,0,1:T(8,128)(2,1)}, u32[]{:S(2)}, u32[]{:S(2)}) async-start(bf16[88,4,352]{2,0,1:T(8,128)(2,1)} %copy.41), calls=%async_computation.6 | async-start | bytes 540672 | tf_op jit(solution)/shard_map/all_to_all | solution.py:35
  34.2 9.3 %all-to-all-start.1 = ((bf16[2,2,88,352]{3,2,1,0:T(8,128)(2,1)}), bf16[2,2,88,352]{3,2,1,0:T(8,128)(2,1)S(1)}, u32[]{:S(2)}, u32[]{:S(2)}) async-start(bf16[2,2,88,352]{3,2,1,0:T(8,128)(2,1)} %bitcast.1), calls=%async_computation.1 | async-start | bytes 540672 | tf_op jit(solution)/shard_map/all_to_all | solution.py:42
  43.5 8.7 %all-to-all-start.4 = ((bf16[2,2,88,352]{3,2,1,0:T(8,128)(2,1)}), bf16[2,2,88,352]{3,2,1,0:T(8,128)(2,1)S(1)}, u32[]{:S(2)}, u32[]{:S(2)}) async-start(bf16[2,2,88,352]{3,2,1,0:T(8,128)(2,1)} %bitcast.8), calls=%async_computation.4 | async-start | bytes 540672 | tf_op jit(solution)/shard_map/all_to_all | solution.py:42
  52.1 8.7 %all-to-all-start.7 = ((bf16[2,2,88,352]{3,2,1,0:T(8,128)(2,1)}), bf16[2,2,88,352]{3,2,1,0:T(8,128)(2,1)S(1)}, u32[]{:S(2)}, u32[]{:S(2)}) async-start(bf16[2,2,88,352]{3,2,1,0:T(8,128)(2,1)} %bitcast.15), calls=%async_computation.7 | async-start | bytes 540672 | tf_op jit(solution)/shard_map/all_to_all | solution.py:42
  60.8 47.1 %all-to-all-start.2 = ((bf16[4,1,1,88,352]{4,3,2,1,0:T(8,128)(2,1)}), bf16[4,1,1,88,352]{4,3,2,1,0:T(8,128)(2,1)S(1)}, u32[]{:S(2)}, u32[]{:S(2)}) async-start(bf16[4,1,1,88,352]{4,3,2,1,0:T(8,128)(2,1)} %bitcast.5), calls=%async_computation.2 | async-start | bytes 540672 | tf_op jit(solution)/shard_map/all_to_all | solution.py:50
  107.9 16.6 %all-to-all-start.5 = ((bf16[4,1,1,88,352]{4,3,2,1,0:T(8,128)(2,1)}), bf16[4,1,1,88,352]{4,3,2,1,0:T(8,128)(2,1)S(1)}, u32[]{:S(2)}, u32[]{:S(2)}) async-start(bf16[4,1,1,88,352]{4,3,2,1,0:T(8,128)(2,1)} %bitcast.12), calls=%async_computation.5 | async-start | bytes 540672 | tf_op jit(solution)/shard_map/all_to_all | solution.py:50
  124.5 17.2 %all-to-all-start.8 = ((bf16[4,1,1,88,352]{4,3,2,1,0:T(8,128)(2,1)}), bf16[4,1,1,88,352]{4,3,2,1,0:T(8,128)(2,1)S(1)}, u32[]{:S(2)}, u32[]{:S(2)}) async-start(bf16[4,1,1,88,352]{4,3,2,1,0:T(8,128)(2,1)} %bitcast.19), calls=%async_computation.8 | async-start | bytes 540672 | tf_op jit(solution)/shard_map/all_to_all | solution.py:50
where the time goes:
time: 155 us; the launch traced here: 154 us
  blocking collectives  71.2 us (46%)
  starting transfers between devices  36.7 us (24%)
  waiting for transfers between devices  31 us (20%)
  local copies, waits for them, and re-layouts  12.5 us (8%)
    psum x1, blocking collectives, shards(): summed = lax.psum(spread, ('dp', 'pipe', 'tensor'))  39.9 us
    all_gather x3, blocking collectives, shards(): lax.all_gather(for_sending(flat_pieces), 'dp', axis=1, tiled=True)  31.3 us
    all_to_all x3, waiting for transfers between devices, shards(): lax.all_to_all(for_sending(grouped), 'pipe', split_axis=0, concat_axis=2,...  14.7 us
    all_to_all x3, starting transfers between devices, shards(): lax.all_to_all(for_sending(routed), 'tensor', split_axis=0, concat_axis=2...  13.7 us
    all_to_all x3, starting transfers between devices, shards(): lax.all_to_all(for_sending(grouped), 'pipe', split_axis=0, concat_axis=2,...  10.5 us
    unnamed x13, local copies, waits for them, and re-layouts  5.65 us
    all_to_all x1, waiting for transfers between devices, shards(): lax.all_to_all(sources[0], 'dp', split_axis=1, concat_axis=0, tiled=True)  5.65 us
    all_to_all x1, waiting for transfers between devices, shards(): lax.all_to_all(sources[2], 'dp', split_axis=1, concat_axis=0, tiled=True)  5.51 us
  transfers between devices with their start and end apart: 9, of which 6 were waited for; matrix products, arithmetic and copies ran while one was open for 6% of the time, Pallas kernels for 0%

commit v1 on v0

--- a/solution.py
+++ b/solution.py
@@ -74,7 +74,9 @@
         * section_hit[None, :, None, None]
         * tile_hit[None, None, :, None]
     )
-    summed = lax.psum(spread, ("dp", "pipe", "tensor"))
+    summed = spread
+    for name in ("dp", ("pipe", "tensor")):
+        summed = lax.psum(summed, name)
     checks = (
         lax.dynamic_slice(summed, (0, lax.axis_index("pipe"), tensor_pos, 0), (3, 1, 1, col_blocks))
         * factor

time: 155 us -> 160 us (1.032)
  blocking collectives: 71.2 us -> 76.4 us
    psum x1 -> x2, blocking collectives: 39.9 us -> 46.7 us  [shards(): summed = lax.psum(summed, name)]
where the time goes in v1:
time: 160 us; the launch traced here: 159 us
  blocking collectives  76.4 us (48%)
  starting transfers between devices  36.6 us (23%)
  waiting for transfers between devices  31 us (19%)
  local copies, waits for them, and re-layouts  12.5 us (8%)
    psum x2, blocking collectives, shards(): summed = lax.psum(summed, name)  46.7 us
    all_gather x3, blocking collectives, shards(): lax.all_gather(for_sending(flat_pieces), 'dp', axis=1, tiled=True)  29.8 us
    all_to_all x3, waiting for transfers between devices, shards(): lax.all_to_all(for_sending(grouped), 'pipe', split_axis=0, concat_axis=2,...  14.7 us
    all_to_all x3, starting transfers between devices, shards(): lax.all_to_all(for_sending(routed), 'tensor', split_axis=0, concat_axis=2...  13.6 us
    all_to_all x3, starting transfers between devices, shards(): lax.all_to_all(for_sending(grouped), 'pipe', split_axis=0, concat_axis=2,...  10.5 us
    all_to_all x1, waiting for transfers between devices, shards(): lax.all_to_all(sources[0], 'dp', split_axis=1, concat_axis=0, tiled=True)  5.65 us
    unnamed x13, local copies, waits for them, and re-layouts  5.65 us
    all_to_all x1, waiting for transfers between devices, shards(): lax.all_to_all(sources[2], 'dp', split_axis=1, concat_axis=0, tiled=True)  5.51 us
  transfers between devices with their start and end apart: 9, of which 6 were waited for; matrix products, arithmetic and copies ran while one was open for 6% of the time, Pallas kernels for 0%

profile of v1, /device:TPU:0, one launch (start us, length us, event | category | flops | bytes accessed | tf_op | source)
XLA Modules:
  0.0 159.2 jit_solution(6410789803808654309)
XLA Ops:
  0.6 0.0 copy-start
  0.7 1.3 all_to_all.90
  1.9 0.7 copy.33
  2.7 4.4 %all-to-all-start = ((bf16[88,4,352]{2,0,1:T(8,128)(2,1)}), bf16[88,4,352]{2,0,1:T(8,128)(2,1)}, u32[]{:S(2)}, u32[]{:S(2)}) async-start(bf16[88,4,352]{2,0,1:T(8,128)(2,1)} %copy.33), calls=%async_computation | async-start | bytes 540672 | tf_op jit(solution)/shard_map/all_to_all | solution.py:33
  7.0 0.3 all_to_all.97
  7.3 0.7 copy.37
  8.1 5.7 %all-to-all-done = bf16[88,4,352]{2,0,1:T(8,128)(2,1)} async-done(((bf16[88,4,352]{2,0,1:T(8,128)(2,1)}), bf16[88,4,352]{2,0,1:T(8,128)(2,1)}, u32[]{:S(2)}, u32[]{:S(2)}) %all-to-all-start) | async-done | bytes 247840 | tf_op jit(solution)/shard_map/all_to_all | solution.py:33
  13.7 4.1 %all-to-all-start.3 = ((bf16[88,4,352]{2,0,1:T(8,128)(2,1)}), bf16[88,4,352]{2,0,1:T(8,128)(2,1)}, u32[]{:S(2)}, u32[]{:S(2)}) async-start(bf16[88,4,352]{2,0,1:T(8,128)(2,1)} %copy.37), calls=%async_computation.3 | async-start | bytes 540672 | tf_op jit(solution)/shard_map/all_to_all | solution.py:34
  17.9 0.3 all_to_all.104
  18.1 0.0 copy-start.4
  18.2 0.7 copy.41
  18.9 5.1 %all-to-all-done.3 = bf16[88,4,352]{2,0,1:T(8,128)(2,1)} async-done(((bf16[88,4,352]{2,0,1:T(8,128)(2,1)}), bf16[88,4,352]{2,0,1:T(8,128)(2,1)}, u32[]{:S(2)}, u32[]{:S(2)}) %all-to-all-start.3) | async-done | bytes 247840 | tf_op jit(solution)/shard_map/all_to_all | solution.py:34
  24.0 4.1 %all-to-all-start.6 = ((bf16[88,4,352]{2,0,1:T(8,128)(2,1)}), bf16[88,4,352]{2,0,1:T(8,128)(2,1)}, u32[]{:S(2)}, u32[]{:S(2)}) async-start(bf16[88,4,352]{2,0,1:T(8,128)(2,1)} %copy.41), calls=%async_computation.6 | async-start | bytes 540672 | tf_op jit(solution)/shard_map/all_to_all | solution.py:35
  28.1 0.0 copy-done
  28.1 0.3 convolution_reduce_fusion.2
  28.4 0.3 convolution_reduce_fusion
  28.7 5.5 %all-to-all-done.6 = bf16[88,4,352]{2,0,1:T(8,128)(2,1)} async-done(((bf16[88,4,352]{2,0,1:T(8,128)(2,1)}), bf16[88,4,352]{2,0,1:T(8,128)(2,1)}, u32[]{:S(2)}, u32[]{:S(2)}) %all-to-all-start.6) | async-done | bytes 247840 | tf_op jit(solution)/shard_map/all_to_all | solution.py:35
  34.2 3.6 %all-to-all-start.1 = ((bf16[2,2,88,352]{3,2,1,0:T(8,128)(2,1)}), bf16[2,2,88,352]{3,2,1,0:T(8,128)(2,1)S(1)}, u32[]{:S(2)}, u32[]{:S(2)}) async-start(bf16[2,2,88,352]{3,2,1,0:T(8,128)(2,1)} %bitcast.1), calls=%async_computation.1 | async-start | bytes 540672 | tf_op jit(solution)/shard_map/all_to_all | solution.py:42
  37.8 0.3 convolution_reduce_fusion.1
  38.1 0.1 bitcast_reduce_fusion.2
  38.3 5.2 %all-to-all-done.1 = bf16[2,2,88,352]{3,2,1,0:T(8,128)(2,1)S(1)} async-done(((bf16[2,2,88,352]{3,2,1,0:T(8,128)(2,1)}), bf16[2,2,88,352]{3,2,1,0:T(8,128)(2,1)S(1)}, u32[]{:S(2)}, u32[]{:S(2)}) %all-to-all-start.1) | async-done | bytes 247840 | tf_op jit(solution)/shard_map/all_to_all | solution.py:42
  43.5 3.4 %all-to-all-start.4 = ((bf16[2,2,88,352]{3,2,1,0:T(8,128)(2,1)}), bf16[2,2,88,352]{3,2,1,0:T(8,128)(2,1)S(1)}, u32[]{:S(2)}, u32[]{:S(2)}) async-start(bf16[2,2,88,352]{3,2,1,0:T(8,128)(2,1)} %bitcast.8), calls=%async_computation.4 | async-start | bytes 540672 | tf_op jit(solution)/shard_map/all_to_all | solution.py:42
  47.0 5.2 %all-to-all-done.4 = bf16[2,2,88,352]{3,2,1,0:T(8,128)(2,1)S(1)} async-done(((bf16[2,2,88,352]{3,2,1,0:T(8,128)(2,1)}), bf16[2,2,88,352]{3,2,1,0:T(8,128)(2,1)S(1)}, u32[]{:S(2)}, u32[]{:S(2)}) %all-to-all-start.4) | async-done | bytes 247840 | tf_op jit(solution)/shard_map/all_to_all | solution.py:42
  52.1 3.4 %all-to-all-start.7 = ((bf16[2,2,88,352]{3,2,1,0:T(8,128)(2,1)}), bf16[2,2,88,352]{3,2,1,0:T(8,128)(2,1)S(1)}, u32[]{:S(2)}, u32[]{:S(2)}) async-start(bf16[2,2,88,352]{3,2,1,0:T(8,128)(2,1)} %bitcast.15), calls=%async_computation.7 | async-start | bytes 540672 | tf_op jit(solution)/shard_map/all_to_all | solution.py:42
  55.6 0.1 broadcast_multiply_fusion.1
  55.7 0.7 copy.34
  56.4 4.4 %all-to-all-done.7 = bf16[2,2,88,352]{3,2,1,0:T(8,128)(2,1)S(1)} async-done(((bf16[2,2,88,352]{3,2,1,0:T(8,128)(2,1)}), bf16[2,2,88,352]{3,2,1,0:T(8,128)(2,1)S(1)}, u32[]{:S(2)}, u32[]{:S(2)}) %all-to-all-start.7) | async-done | bytes 247840 | tf_op jit(solution)/shard_map/all_to_all | solution.py:42
  60.8 5.1 %all-to-all-start.2 = ((bf16[4,1,1,88,352]{4,3,2,1,0:T(8,128)(2,1)}), bf16[4,1,1,88,352]{4,3,2,1,0:T(8,128)(2,1)S(1)}, u32[]{:S(2)}, u32[]{:S(2)}) async-start(bf16[4,1,1,88,352]{4,3,2,1,0:T(8,128)(2,1)} %bitcast.5), calls=%async_computation.2 | async-start | bytes 540672 | tf_op jit(solution)/shard_map/all_to_all | solution.py:50
  65.9 0.1 broadcast_multiply_fusion
  66.0 10.4 %psum.14 = f32[3,2,4,11]{3,2,1,0:T(4,128)S(1)} all-reduce(f32[3,2,4,11]{3,2,1,0:T(4,128)S(1)} %broadcast_multiply_fusion), channel_id=1, replica_groups=mesh['dp'=4,'pipe'=2,'tensor'=4] {'dp'}, use_global_device_ids=true, to_apply=%region_3.4 | all-reduce | flops 264 | bytes 2112 | tf_op jit(solution)/shard_map/psum | solution.py:79
  76.4 36.2 %psum.15 = f32[3,2,4,11]{3,2,1,0:T(4,128)S(1)} all-reduce(f32[3,2,4,11]{3,2,1,0:T(4,128)S(1)} %psum.14), channel_id=1, replica_groups=mesh['dp'=4,'pipe'=2,'tensor'=4] {'pipe','tensor'}, use_global_device_ids=true, to_apply=%region_4.5 | all-reduce | flops 264 | bytes 2112 | tf_op jit(solution)/shard_map/psum | solution.py:79
  112.6 0.6 dynamic-slice_multiply_fusion
  113.2 0.7 copy.38
  113.9 0.7 copy.42
  114.7 0.0 all-to-all-done.2
  114.7 3.5 %all-to-all-start.5 = ((bf16[4,1,1,88,352]{4,3,2,1,0:T(8,128)(2,1)}), bf16[4,1,1,88,352]{4,3,2,1,0:T(8,128)(2,1)S(1)}, u32[]{:S(2)}, u32[]{:S(2)}) async-start(bf16[4,1,1,88,352]{4,3,2,1,0:T(8,128)(2,1)} %bitcast.12), calls=%async_computation.5 | async-start | bytes 540672 | tf_op jit(solution)/shard_map/all_to_all | solution.py:50
  118.1 0.2 copy.36
  118.3 9.3 %all_gather.9 = bf16[352,1408]{0,1:T(8,128)(2,1)S(1)} all-gather(bf16[352,352]{0,1:T(8,128)(2,1)S(1)} %copy.36), channel_id=1, replica_groups=mesh['dp'=4,'pipe'=2,'tensor'=4] {'dp'}, dimensions={1}, use_global_device_ids=true | all-gather | bytes 1239040 | tf_op jit(solution)/shard_map/all_gather | solution.py:56
  127.7 1.9 %copy.45 = bf16[352,1408]{1,0:T(8,128)(2,1)} copy(bf16[352,1408]{0,1:T(8,128)(2,1)S(1)} %all_gather.9) | data formatting | bytes 1982464
  129.6 0.0 all-to-all-done.5
  129.6 5.1 %all-to-all-start.8 = ((bf16[4,1,1,88,352]{4,3,2,1,0:T(8,128)(2,1)}), bf16[4,1,1,88,352]{4,3,2,1,0:T(8,128)(2,1)S(1)}, u32[]{:S(2)}, u32[]{:S(2)}) async-start(bf16[4,1,1,88,352]{4,3,2,1,0:T(8,128)(2,1)} %bitcast.19), calls=%async_computation.8 | async-start | bytes 540672 | tf_op jit(solution)/shard_map/all_to_all | solution.py:50
  134.6 0.2 copy.40
  134.8 10.1 %all_gather.10 = bf16[352,1408]{0,1:T(8,128)(2,1)S(1)} all-gather(bf16[352,352]{0,1:T(8,128)(2,1)S(1)} %copy.40), channel_id=1, replica_groups=mesh['dp'=4,'pipe'=2,'tensor'=4] {'dp'}, dimensions={1}, use_global_device_ids=true | all-gather | bytes 1239040 | tf_op jit(solution)/shard_map/all_gather | solution.py:56
  144.9 1.9 %copy.46 = bf16[352,1408]{1,0:T(8,128)(2,1)} copy(bf16[352,1408]{0,1:T(8,128)(2,1)S(1)} %all_gather.10) | data formatting | bytes 1982464
  146.8 0.0 all-to-all-done.8
  146.8 0.2 copy.44
  147.0 10.3 %all_gather.11 = bf16[352,1408]{0,1:T(8,128)(2,1)S(1)} all-gather(bf16[352,352]{0,1:T(8,128)(2,1)S(1)} %copy.44), channel_id=1, replica_groups=mesh['dp'=4,'pipe'=2,'tensor'=4] {'dp'}, dimensions={1}, use_global_device_ids=true | all-gather | bytes 1239040 | tf_op jit(solution)/shard_map/all_gather | solution.py:56
  157.3 1.9 %copy.47 = bf16[352,1408]{1,0:T(8,128)(2,1)} copy(bf16[352,1408]{0,1:T(8,128)(2,1)S(1)} %all_gather.11) | data formatting | bytes 1982464
  (10 shorter events, 0.0 us)
Async XLA Ops:
  0.6 27.4 %copy-start = (f32[1408]{0:T(1024)S(1)}, f32[1408]{0:T(1024)}, u32[]{:S(2)}) copy-start(f32[1408]{0:T(1024)} %param.8) | copy-start | bytes 16900
  0.6 6.4 %copy-start.3 = (bf16[88,1408]{1,0:T(8,128)(2,1)S(1)}, bf16[88,1408]{1,0:T(8,128)(2,1)}, u32[]{:S(2)}) copy-start(bf16[88,1408]{1,0:T(8,128)(2,1)} %param.6) | copy-start | bytes 743428
  2.7 15.2 %copy-start.2 = (bf16[88,1408]{1,0:T(8,128)(2,1)S(1)}, bf16[88,1408]{1,0:T(8,128)(2,1)}, u32[]{:S(2)}) copy-start(bf16[88,1408]{1,0:T(8,128)(2,1)} %param.7) | copy-start | bytes 743428
  2.7 11.1 %all-to-all-start = ((bf16[88,4,352]{2,0,1:T(8,128)(2,1)}), bf16[88,4,352]{2,0,1:T(8,128)(2,1)}, u32[]{:S(2)}, u32[]{:S(2)}) async-start(bf16[88,4,352]{2,0,1:T(8,128)(2,1)} %copy.33), calls=%async_computation | async-start | bytes 540672 | tf_op jit(solution)/shard_map/all_to_all | solution.py:33
  8.1 20.0 %copy-start.1 = (bf16[88,1408]{1,0:T(8,128)(2,1)S(1)}, bf16[88,1408]{1,0:T(8,128)(2,1)}, u32[]{:S(2)}) copy-start(bf16[88,1408]{1,0:T(8,128)(2,1)} %param.5) | copy-start | bytes 743428
  13.7 10.3 %all-to-all-start.3 = ((bf16[88,4,352]{2,0,1:T(8,128)(2,1)}), bf16[88,4,352]{2,0,1:T(8,128)(2,1)}, u32[]{:S(2)}, u32[]{:S(2)}) async-start(bf16[88,4,352]{2,0,1:T(8,128)(2,1)} %copy.37), calls=%async_computation.3 | async-start | bytes 540672 | tf_op jit(solution)/shard_map/all_to_all | solution.py:34
  18.1 20.0 %copy-start.4 = (f32[1408]{0:T(1024)S(1)}, f32[1408]{0:T(1024)}, u32[]{:S(2)}) copy-start(f32[1408]{0:T(1024)} %param.9) | copy-start | bytes 16900
  24.0 10.2 %all-to-all-start.6 = ((bf16[88,4,352]{2,0,1:T(8,128)(2,1)}), bf16[88,4,352]{2,0,1:T(8,128)(2,1)}, u32[]{:S(2)}, u32[]{:S(2)}) async-start(bf16[88,4,352]{2,0,1:T(8,128)(2,1)} %copy.41), calls=%async_computation.6 | async-start | bytes 540672 | tf_op jit(solution)/shard_map/all_to_all | solution.py:35
  34.2 9.3 %all-to-all-start.1 = ((bf16[2,2,88,352]{3,2,1,0:T(8,128)(2,1)}), bf16[2,2,88,352]{3,2,1,0:T(8,128)(2,1)S(1)}, u32[]{:S(2)}, u32[]{:S(2)}) async-start(bf16[2,2,88,352]{3,2,1,0:T(8,128)(2,1)} %bitcast.1), calls=%async_computation.1 | async-start | bytes 540672 | tf_op jit(solution)/shard_map/all_to_all | solution.py:42
  43.5 8.7 %all-to-all-start.4 = ((bf16[2,2,88,352]{3,2,1,0:T(8,128)(2,1)}), bf16[2,2,88,352]{3,2,1,0:T(8,128)(2,1)S(1)}, u32[]{:S(2)}, u32[]{:S(2)}) async-start(bf16[2,2,88,352]{3,2,1,0:T(8,128)(2,1)} %bitcast.8), calls=%async_computation.4 | async-start | bytes 540672 | tf_op jit(solution)/shard_map/all_to_all | solution.py:42
  52.1 8.7 %all-to-all-start.7 = ((bf16[2,2,88,352]{3,2,1,0:T(8,128)(2,1)}), bf16[2,2,88,352]{3,2,1,0:T(8,128)(2,1)S(1)}, u32[]{:S(2)}, u32[]{:S(2)}) async-start(bf16[2,2,88,352]{3,2,1,0:T(8,128)(2,1)} %bitcast.15), calls=%async_computation.7 | async-start | bytes 540672 | tf_op jit(solution)/shard_map/all_to_all | solution.py:42
  60.8 53.9 %all-to-all-start.2 = ((bf16[4,1,1,88,352]{4,3,2,1,0:T(8,128)(2,1)}), bf16[4,1,1,88,352]{4,3,2,1,0:T(8,128)(2,1)S(1)}, u32[]{:S(2)}, u32[]{:S(2)}) async-start(bf16[4,1,1,88,352]{4,3,2,1,0:T(8,128)(2,1)} %bitcast.5), calls=%async_computation.2 | async-start | bytes 540672 | tf_op jit(solution)/shard_map/all_to_all | solution.py:50
  114.7 14.9 %all-to-all-start.5 = ((bf16[4,1,1,88,352]{4,3,2,1,0:T(8,128)(2,1)}), bf16[4,1,1,88,352]{4,3,2,1,0:T(8,128)(2,1)S(1)}, u32[]{:S(2)}, u32[]{:S(2)}) async-start(bf16[4,1,1,88,352]{4,3,2,1,0:T(8,128)(2,1)} %bitcast.12), calls=%async_computation.5 | async-start | bytes 540672 | tf_op jit(solution)/shard_map/all_to_all | solution.py:50
  129.6 17.2 %all-to-all-start.8 = ((bf16[4,1,1,88,352]{4,3,2,1,0:T(8,128)(2,1)}), bf16[4,1,1,88,352]{4,3,2,1,0:T(8,128)(2,1)S(1)}, u32[]{:S(2)}, u32[]{:S(2)}) async-start(bf16[4,1,1,88,352]{4,3,2,1,0:T(8,128)(2,1)} %bitcast.19), calls=%async_computation.8 | async-start | bytes 540672 | tf_op jit(solution)/shard_map/all_to_all | solution.py:50
